TPU v7x, 512 devices: a 8x2x16 block of a 8x8x16 slice. The times are simulated.
512 devices in a mesh: groups: 2 (over y), ctx: 32 (over z, core), tp: 8 (over x).
Axes of the slice: x: 8, y: 2, z: 16, core: 2. Of those that a mesh axis runs over, the one named last changes fastest.
The devices are a block of a 8x8x16 slice.
Arguments:
- query_matrix: bfloat16 [8192, 8192], P(('groups', 'ctx'), 'tp'), parts along dimension 0, may hold values from -20 to 20
- key_matrix: bfloat16 [8192, 1024], P(('groups', 'ctx'), 'tp'), parts along dimension 0, may hold values from -20 to 20
- value_matrix: bfloat16 [8192, 1024], P(('groups', 'ctx'), 'tp'), parts along dimension 0, may hold values from -6 to 6
- doc_ids: int32 [8192], P('groups'), parts along dimension 0, may hold values from 0 to 5, never falling along the last dimension, each value on 1 to 2048 neighbouring positions
- out_weight: bfloat16 [8192, 4096], P('tp', 'ctx'), may hold values from -0.0625 to 0.0625
Outputs:
- projected: bfloat16 [8192, 4096], P(('groups', 'ctx'), 'tp'), parts along dimension 0
There are 2 independent parts, one for each index of `groups`. A program takes and returns all parts, laid end to end along the dimension named above; an argument that names none is the same for every part. Nothing has to cross between parts.
Inputs may be any that keep to these rules, and one draw needn't show every extreme that they name: `doc_ids`: non-decreasing along the sequence; each document holds 1 to 2048 tokens, one exactly 2048.
All inputs are finite; a program needn't handle non-finite values.
Results may differ from a plain program's by a relative error of at most 0.015.
Values may be sent and summed in bfloat16 or wider, within the bound.
No kernel may reach another device: no remote copies, remote signals or barrier semaphores. Data moves between devices by JAX's collectives and lax.ppermute only.
A program may use at most 64 MiB of HBM per device.

v0:
```python
import math
import jax
import jax.numpy as jnp
from jax import lax
from jax.sharding import PartitionSpec as P

HEAD_SIZE = 128
rope_base = 1000000.0


def in_one_piece(arrays, axis, dim, along):
    ends, at = ([], 0)
    for a in arrays[:-1]:
        at += a.shape[along]
        ends.append(at)
    both = jnp.concatenate(arrays, axis=along)
    return tuple(jnp.split(lax.all_gather(both, axis, axis=dim, tiled=True), ends, axis=along))


def split_up(x, dim, size):
    lengths = x.shape
    pieces = x.reshape(*lengths[:dim], size, lengths[dim] // size, *lengths[dim + 1 :])
    return jnp.moveaxis(pieces, dim, 0)


def sent_and_summed(x, axis, dim):
    pieces = split_up(x, dim, lax.axis_size(axis))
    arrived = lax.all_to_all(pieces, axis, split_axis=0, concat_axis=0, tiled=True)
    return arrived.astype(jnp.float32).sum(axis=0)


def rotary_tables(rows, token_positions, heads):
    half_dim = HEAD_SIZE // 2
    frequency = jnp.power(
        jnp.float32(rope_base), -jnp.arange(half_dim, dtype=jnp.float32) * (2.0 / HEAD_SIZE)
    )
    angles = token_positions.astype(jnp.float32)[:, None] * frequency[None, :]
    cosine = jnp.cos(angles)[:, None, :]
    sine = jnp.sin(angles)[:, None, :]
    values = rows.astype(jnp.float32).reshape(rows.shape[0], heads, HEAD_SIZE)
    first = values[..., :half_dim]
    second = values[..., half_dim:]
    turned = jnp.concatenate([first * cosine - second * sine, second * cosine + first * sine], -1)
    return turned.reshape(rows.shape[0], heads * HEAD_SIZE).astype(jnp.bfloat16)


def keep_state(held_state, unused_block):
    return held_state


def on_device(query_matrix, key_matrix, value_matrix, doc_ids, out_weight):
    ctx_index = lax.axis_index("ctx")
    tok_rows = query_matrix.shape[0]
    query_heads = query_matrix.shape[1] // HEAD_SIZE
    key_heads = key_matrix.shape[1] // HEAD_SIZE
    group_width = query_heads // key_heads
    inverse_root = HEAD_SIZE ** (-0.5)
    local_rows = jnp.arange(tok_rows, dtype=jnp.int32)
    given_pos = ctx_index * tok_rows + local_rows
    query_matrix_rot = rotary_tables(query_matrix, given_pos, query_heads)
    keys_here = rotary_tables(key_matrix, given_pos, key_heads)
    query_doc = jnp.take(doc_ids, given_pos, axis=0)
    query_four = query_matrix_rot.reshape(tok_rows, key_heads, group_width, HEAD_SIZE)
    first_doc = jnp.min(query_doc)
    last_doc = jnp.max(query_doc)
    last_pos = jnp.max(given_pos)

    def attend(state, block):
        key_block, value_block, doc_block, pos_block = block
        row_max, totals, accum = state
        scores = (
            jnp.einsum("qkgd,skd->kgqs", query_four, key_block, preferred_element_type=jnp.float32)
            * inverse_root
        )
        allowed = (
            (query_doc[:, None] == doc_block[None, :]) & (pos_block[None, :] <= given_pos[:, None])
        )[None, None]
        new_max = jnp.maximum(row_max, jnp.max(jnp.where(allowed, scores, -1e30), -1))
        weights = jnp.where(allowed, jnp.exp(scores - new_max[..., None]), 0.0)
        factor = jnp.exp(row_max - new_max)
        totals = totals * factor + jnp.sum(weights, -1)
        accum = accum * jnp.transpose(factor, (2, 0, 1))[..., None] + jnp.einsum(
            "kgqs,skd->qkgd",
            weights.astype(jnp.bfloat16),
            value_block,
            preferred_element_type=jnp.float32,
        )
        return (new_max, totals, accum)

    start_state = (
        jnp.full((key_heads, group_width, tok_rows), -1e30, jnp.float32),
        jnp.zeros((key_heads, group_width, tok_rows), jnp.float32),
        jnp.zeros((tok_rows, key_heads, group_width, HEAD_SIZE), jnp.float32),
    )
    key_piece, value_piece = in_one_piece((keys_here, value_matrix), "ctx", 0, 1)
    count = key_piece.shape[0]
    block_rows = math.gcd(count, 512)
    block_count = count // block_rows
    positions = jnp.arange(count, dtype=jnp.int32)
    blocks = (
        key_piece.reshape(block_count, block_rows, key_heads, HEAD_SIZE),
        value_piece.reshape(block_count, block_rows, key_heads, HEAD_SIZE),
        jnp.take(doc_ids, positions, axis=0).reshape(block_count, block_rows),
        positions.reshape(block_count, block_rows),
    )

    def step_block(inner_state, block):
        live = (
            (jnp.min(block[3]) <= last_pos)
            & (jnp.min(block[2]) <= last_doc)
            & (jnp.max(block[2]) >= first_doc)
        )
        return (lax.cond(live, attend, keep_state, inner_state, block), None)

    final_state, unused_out = lax.scan(step_block, start_state, blocks)
    row_max, totals, accum = final_state
    attention = (
        (accum / jnp.transpose(totals, (2, 0, 1))[..., None])
        .reshape(tok_rows, query_heads * HEAD_SIZE)
        .astype(jnp.bfloat16)
    )
    terms = jnp.dot(
        attention,
        lax.all_gather(out_weight, "ctx", axis=1, tiled=True),
        preferred_element_type=jnp.float32,
    )
    return sent_and_summed(terms.astype(jnp.bfloat16), "tp", 1).astype(jnp.bfloat16)


def solution(mesh):
    in_specs = (
        P(("groups", "ctx"), "tp"),
        P(("groups", "ctx"), "tp"),
        P(("groups", "ctx"), "tp"),
        P("groups"),
        P("tp", "ctx"),
    )
    out_specs = P(("groups", "ctx"), "tp")
    return jax.shard_map(
        on_device, mesh=mesh, in_specs=in_specs, out_specs=out_specs, check_vma=False
    )
```

profile of v0, /device:TPU:65, one launch (start us, length us, event | category | flops | bytes accessed | tf_op | source)
XLA Modules:
  0.0 262.6 jit_solution(11426903617318993670)
XLA Ops:
  6.5 0.0 copy-start
  6.6 0.0 all-gather.3.cloned.1.call-start
  6.6 0.6 fusion.36
  7.2 0.9 copy.19
  8.1 0.9 copy.20
  8.9 0.2 fusion.32
  9.2 0.6 pad_maximum_fusion.1
  9.8 0.1 all-gather.3.cloned.1.call-update
  9.9 0.1 all-gather.5.cloned.1.call-start
  9.9 0.7 all-gather.5.cloned.1.call-update
  10.7 1.1 copy.21
  11.8 0.2 multiply_cosine_fusion
  12.0 0.1 fusion.25
  12.1 0.2 copy.24
  12.4 0.0 copy-done
  12.4 1.1 gather_fusion.1
  13.5 23.0 %gather_fusion = s32[4096]{0:T(1024)S(1)} fusion(s32[4096]{0:T(1024)S(1)} %copy-done, s32[4096]{0:T(1024)S(1)} %iota_clamp_fusion), kind=kCustom, calls=%fused_computation | custom fusion | bytes 49152 | tf_op jit(solution)/shard_map/jit(_take)/gather | solution.py:103
  36.6 0.7 fusion.39
  37.3 82.9 %all-gather.3.cloned.1.call-done = bf16[4096,256]{0,1:T(8,128)(2,1)} async-done(((bf16[128,256]{0,1:T(8,128)(2,1)}), bf16[4096,256]{0,1:T(8,128)(2,1)}) %all-gather.3.cloned.1.call-update) | async-done | bytes 2097168 | tf_op jit(solution)/shard_map/all_gather | solution.py:17
  120.2 1.7 fusion.41
  121.9 0.7 copy.22
  122.6 0.5 copy.25
  123.1 0.7 copy.28
  123.8 37.2 %while.15 = (s32[]{:T(128)}, f32[1,8,128]{2,1,0:T(8,128)S(1)}, f32[1,8,128]{2,1,0:T(8,128)S(1)}, f32[128,1,8,128]{0,3,2,1:T(8,128)S(1)}, s32[8,512]{1,0:T(8,128)...) while((s32[]{:T(128)}, f32[1,8,128]{2,1,0:T(8,128)S(1)}, ...), condition=%wide.region_11.12_spmd.clone, body=%wide.region_3.11_spmd.clone.sunk | while | flops 274666112 | bytes 8207207 | solution.py:115
  123.9 0.7 fusion.45
  128.2 1.8 conditional.3
  128.3 0.2 compare_and_fusion
  128.5 0.5 fusion.2
  129.0 0.4 fusion.6
  129.4 0.6 fusion.7
  130.1 0.7 fusion.45
  134.5 0.7 fusion.45
  138.9 0.7 fusion.45
  143.3 0.7 fusion.45
  147.8 0.7 fusion.45
  152.2 0.7 fusion.45
  156.6 0.7 fusion.45
  161.0 0.1 divide_convert_fusion
  161.1 54.5 %all-gather.5.cloned.1.call-done = bf16[1024,4096]{1,0:T(8,128)(2,1)} async-done(((bf16[1024,128]{1,0:T(8,128)(2,1)}), bf16[1024,4096]{1,0:T(8,128)(2,1)}) %all-gather.5.cloned.1.call-update) | async-done | bytes 8388624 | tf_op jit(solution)/shard_map/all_gather | solution.py:124
  215.6 4.7 %convolution_convert_fusion = bf16[128,4096]{1,0:T(8,128)(2,1)S(1)} fusion(bf16[128,1024]{0,1:T(8,128)(2,1)S(1)} %bitcast.90, bf16[1024,4096]{1,0:T(8,128)(2,1)} %all-gather.5.cloned.1.call-done), kind=kOutput, calls=%fused_computation.35 | convolution fusion | flops 1074266112 | bytes 9699328 | tf_op jit(solution)/shard_map/dot_general | solution.py:122
  220.2 0.1 copy.31
  220.3 34.6 %all_to_all.5 = bf16[8,128,512]{2,1,0:T(8,128)(2,1)S(1)} all-to-all(bf16[8,128,512]{2,1,0:T(8,128)(2,1)S(1)} %bitcast.85), channel_id=1, replica_groups=mesh['groups'=2,'ctx'=32,'tp'=8] {'tp'}, dimensions={0} | all-to-all | bytes 2097152 | tf_op jit(solution)/shard_map/all_to_all | solution.py:28
  254.9 0.8 reduce_sum.23
  (32 shorter events, 0.3 us)
Async XLA Ops:
  6.5 5.8 %copy-start = (s32[4096]{0:T(1024)S(1)}, s32[4096]{0:T(1024)}, u32[]{:S(2)}) copy-start(s32[4096]{0:T(1024)} %param.12) | copy-start | bytes 49156
  6.6 113.7 %all-gather.3.cloned.1.call-start = ((), (), s32[]{:S(2)}) async-start(), calls=%async_computation.1 | async-start | bytes 2162688 | tf_op jit(solution)/shard_map/all_gather | solution.py:17
  9.9 205.7 %all-gather.5.cloned.1.call-start = ((), (), s32[]{:S(2)}) async-start(), calls=%async_computation.2 | async-start | bytes 8650752 | tf_op jit(solution)/shard_map/all_gather | solution.py:124
Sparse Core Ops, SparseCore 0:
  10.0 110.2 all-gather.2
  122.3 93.2 all-gather.4
where the time goes:
time: 263 us
  waiting for transfers between devices  138 us (52%)
  blocking collectives  34.6 us (13%)
  local copies, waits for them, and re-layouts  30.9 us (12%)
  loops' own time  29.9 us (11%)
  between operations  13.6 us (5%)
  other arithmetic  9.57 us (4%)
  matrix products  5.76 us (2%)
    all_gather x1, waiting for transfers between devices, in_one_piece(): lax.all_gather(both, axis, axis=dim, tiled=True)  82.9 us
    all_gather x1, waiting for transfers between devices, on_device(): lax.all_gather(out_weight, 'ctx', axis=1, tiled=True)  54.5 us
    all_to_all x1, blocking collectives, sent_and_summed(): lax.all_to_all(pieces, axis, split_axis=0, concat_axis=0, tiled=True)  34.6 us
    another operation x1, loops' own time, on_device(): final_state, unused_out = lax.scan(step_block, start_state, blocks)  29.7 us
    gather x2, local copies, waits for them, and re-layouts, on_device(): jnp.take(doc_ids, positions, axis=0).reshape(block_count, block_rows)  23 us
    reduce_max x8, other arithmetic, step_block(): jnp.max(block[2]) >= first_doc  5.52 us
  transfers between devices with their start and end apart: 2, of which 2 were waited for; matrix products, arithmetic and copies ran while one was open for 14% of the time, Pallas kernels for 0%

commit v1 on v0

--- a/solution.py
+++ b/solution.py
@@ -6,6 +6,11 @@
 
 HEAD_SIZE = 128
 rope_base = 1000000.0
+
+
+def gather_from_all(x, axis, dim):
+    copies = jnp.concatenate([x] * lax.axis_size(axis), axis=dim)
+    return lax.all_to_all(copies, axis, dim, dim, tiled=True)
 
 
 def in_one_piece(arrays, axis, dim, along):
@@ -120,9 +125,7 @@
         .astype(jnp.bfloat16)
     )
     terms = jnp.dot(
-        attention,
-        lax.all_gather(out_weight, "ctx", axis=1, tiled=True),
-        preferred_element_type=jnp.float32,
+        attention, gather_from_all(out_weight, "ctx", 1), preferred_element_type=jnp.float32
     )
     return sent_and_summed(terms.astype(jnp.bfloat16), "tp", 1).astype(jnp.bfloat16)
 

time: 263 us -> 508 us (1.93); the launches traced: 263 us -> 500 us
  waiting for transfers between devices: 138 us -> 302 us
  starting transfers between devices: 0.07 us -> 46.4 us
  local copies, waits for them, and re-layouts: 30.9 us -> 57.1 us
    all_to_all x0 -> x1, waiting for transfers between devices: none -> 176 us  [gather_from_all(): return lax.all_to_all(copies, axis, dim, dim, tiled=True)]
    all_gather x1 -> x0, waiting for transfers between devices: 54.5 us -> none  [on_device(): lax.all_gather(out_weight, 'ctx', axis=1, tiled=True)]
    all_to_all x0 -> x1, starting transfers between devices: none -> 46.3 us  [gather_from_all(): return lax.all_to_all(copies, axis, dim, dim, tiled=True)]
    all_gather x1, waiting for transfers between devices: 82.9 us -> 126 us  [in_one_piece(): lax.all_gather(both, axis, axis=dim, tiled=True)]
    all_to_all x0 -> x2, local copies, waits for them, and re-layouts: none -> 23.7 us  [gather_from_all(): return lax.all_to_all(copies, axis, dim, dim, tiled=True)]
  transfers between devices with their start and end apart: 2 -> 2, of which waited for: 2 -> 2; matrix products, arithmetic and copies ran while one was open for 14% -> 8% of each run, Pallas kernels for 0% -> 0%
where the time goes in v1:
time: 508 us; the launch traced here: 500 us
  waiting for transfers between devices  302 us (59%)
  local copies, waits for them, and re-layouts  57.1 us (11%)
  starting transfers between devices  46.4 us (9%)
  blocking collectives  33.7 us (7%)
  loops' own time  29.9 us (6%)
  between operations  13.9 us (3%)
  other arithmetic  10.1 us (2%)
  matrix products  7.37 us (1%)
    all_to_all x1, waiting for transfers between devices, gather_from_all(): return lax.all_to_all(copies, axis, dim, dim, tiled=True)  176 us
    all_gather x1, waiting for transfers between devices, in_one_piece(): lax.all_gather(both, axis, axis=dim, tiled=True)  126 us
    all_to_all x1, starting transfers between devices, gather_from_all(): return lax.all_to_all(copies, axis, dim, dim, tiled=True)  46.3 us
    all_to_all x1, blocking collectives, sent_and_summed(): lax.all_to_all(pieces, axis, split_axis=0, concat_axis=0, tiled=True)  33.7 us
    another operation x1, loops' own time, on_device(): final_state, unused_out = lax.scan(step_block, start_state, blocks)  29.7 us
    all_to_all x2, local copies, waits for them, and re-layouts, gather_from_all(): return lax.all_to_all(copies, axis, dim, dim, tiled=True)  23.7 us
    gather x2, local copies, waits for them, and re-layouts, on_device(): jnp.take(doc_ids, positions, axis=0).reshape(block_count, block_rows)  23 us
  transfers between devices with their start and end apart: 2, of which 2 were waited for; matrix products, arithmetic and copies ran while one was open for 8% of the time, Pallas kernels for 0%

profile of v1, /device:TPU:65, one launch (start us, length us, event | category | flops | bytes accessed | tf_op | source)
XLA Modules:
  0.0 500.2 jit_solution(14058825310169833204)
XLA Ops:
  6.5 0.0 copy-start
  6.6 1.1 copy.66
  8.5 0.0 copy-start.1
  8.5 3.2 copy-done.1
  11.8 11.9 %copy.98 = bf16[1024,32,128]{2,0,1:T(8,128)(2,1)} copy(bf16[1024,32,128]{0,2,1:T(8,128)(2,1)} %bitcast.87) | data formatting | bytes 16777216 | tf_op jit(solution)/shard_map/all_to_all | solution.py:13
  23.6 0.0 copy-start.3
  23.6 0.0 copy-start.4
  23.6 0.0 copy-start.2
  23.6 46.3 %all-to-all-start = ((bf16[1024,32,128]{2,0,1:T(8,128)(2,1)}), bf16[1024,32,128]{2,0,1:T(8,128)(2,1)}, u32[]{:S(2)}, u32[]{:S(2)}) async-start(bf16[1024,32,128]{2,0,1:T(8,128)(2,1)} %copy.98), calls=%async_computation | async-start | bytes 16777216 | tf_op jit(solution)/shard_map/all_to_all | solution.py:13
  69.9 0.1 all-gather.2.cloned.1.call-start
  70.0 0.0 copy-done.3
  70.0 0.1 copy.59
  70.1 0.0 copy-done.4
  70.1 0.1 copy.60
  70.3 0.6 fusion.36
  70.9 0.2 fusion.32
  71.2 0.6 pad_maximum_fusion.1
  71.8 0.1 all-gather.2.cloned.1.call-update
  71.8 0.0 copy-done.2
  71.9 0.2 copy.61
  72.1 0.2 multiply_cosine_fusion
  72.3 0.1 fusion.25
  72.4 0.2 copy.64
  72.6 0.0 copy-done
  72.6 1.1 gather_fusion.1
  73.8 23.0 %gather_fusion = s32[4096]{0:T(1024)S(1)} fusion(s32[4096]{0:T(1024)S(1)} %copy-done, s32[4096]{0:T(1024)S(1)} %iota_clamp_fusion), kind=kCustom, calls=%fused_computation | custom fusion | bytes 49152 | tf_op jit(solution)/shard_map/jit(_take)/gather | solution.py:108
  96.8 0.6 fusion.39
  97.5 125.6 %all-gather.2.cloned.1.call-done = bf16[4096,256]{0,1:T(8,128)(2,1)} async-done(((bf16[128,256]{0,1:T(8,128)(2,1)}), bf16[4096,256]{0,1:T(8,128)(2,1)}) %all-gather.2.cloned.1.call-update) | async-done | bytes 2097168 | tf_op jit(solution)/shard_map/all_gather | solution.py:22
  223.1 1.7 fusion.41
  224.7 0.7 copy.62
  225.4 0.5 copy.65
  225.9 0.7 copy.102
  226.7 37.7 %while.15 = (s32[]{:T(128)}, f32[1,8,128]{2,1,0:T(8,128)S(1)}, f32[1,8,128]{2,1,0:T(8,128)S(1)}, f32[128,1,8,128]{0,3,2,1:T(8,128)S(1)}, s32[8,512]{1,0:T(8,128)...) while((s32[]{:T(128)}, f32[1,8,128]{2,1,0:T(8,128)S(1)}, ...), condition=%wide.region_11.12_spmd.clone, body=%wide.region_3.11_spmd.clone.sunk | while | flops 274666112 | bytes 8207207 | solution.py:120
  226.7 0.8 fusion.45
  231.1 1.8 conditional.3
  231.2 0.2 compare_and_fusion
  231.4 0.5 fusion.2
  231.9 0.4 fusion.6
  232.3 0.6 fusion.7
  233.0 0.8 fusion.45
  237.5 0.8 fusion.45
  242.0 0.8 fusion.45
  246.5 0.8 fusion.45
  250.9 0.8 fusion.45
  255.4 0.8 fusion.45
  259.9 0.8 fusion.45
  264.4 0.1 divide_convert_fusion
  264.5 176.1 %all-to-all-done = bf16[1024,32,128]{2,0,1:T(8,128)(2,1)} async-done(((bf16[1024,32,128]{2,0,1:T(8,128)(2,1)}), bf16[1024,32,128]{2,0,1:T(8,128)(2,1)}, u32[]{:S(2)}, u32[]{:S(2)}) %all-to-all-start) | async-done | bytes 8388640 | tf_op jit(solution)/shard_map/all_to_all | solution.py:13
  440.6 11.9 %copy.99 = bf16[1024,32,128]{0,2,1:T(8,128)(2,1)} copy(bf16[1024,32,128]{2,0,1:T(8,128)(2,1)} %all-to-all-done) | data formatting | bytes 16777216 | tf_op jit(solution)/shard_map/all_to_all | solution.py:13
  452.4 6.3 %convolution_convert_fusion = bf16[128,4096]{1,0:T(8,128)(2,1)S(1)} fusion(bf16[128,1024]{0,1:T(8,128)(2,1)S(1)} %bitcast.94, bf16[1024,4096]{0,1:T(8,128)(2,1)} %bitcast.86), kind=kOutput, calls=%fused_computation.35 | convolution fusion | flops 1074266112 | bytes 9699328 | tf_op jit(solution)/shard_map/dot_general | solution.py:127
  458.7 0.1 copy.105
  458.8 33.7 %all_to_all.17 = bf16[8,128,512]{2,1,0:T(8,128)(2,1)S(1)} all-to-all(bf16[8,128,512]{2,1,0:T(8,128)(2,1)S(1)} %bitcast.90), channel_id=1, replica_groups=mesh['groups'=2,'ctx'=32,'tp'=8] {'tp'}, dimensions={0} | all-to-all | bytes 2097152 | tf_op jit(solution)/shard_map/all_to_all | solution.py:33
  492.5 0.8 reduce_sum.23
  (64 shorter events, 0.9 us)
Async XLA Ops:
  6.5 66.1 %copy-start = (s32[4096]{0:T(1024)S(1)}, s32[4096]{0:T(1024)}, u32[]{:S(2)}) copy-start(s32[4096]{0:T(1024)} %param.12) | copy-start | bytes 49156
  8.5 3.2 copy-start.1
  23.6 46.4 %copy-start.3 = (bf16[128,128]{1,0:T(8,128)(2,1)S(1)}, bf16[128,128]{1,0:T(8,128)(2,1)}, u32[]{:S(2)}) copy-start(bf16[128,128]{1,0:T(8,128)(2,1)} %param.10) | copy-start | bytes 98308
  23.6 46.5 %copy-start.4 = (bf16[128,128]{1,0:T(8,128)(2,1)S(1)}, bf16[128,128]{1,0:T(8,128)(2,1)}, u32[]{:S(2)}) copy-start(bf16[128,128]{1,0:T(8,128)(2,1)} %param.11) | copy-start | bytes 98308
  23.6 48.2 %copy-start.2 = (bf16[128,1024]{1,0:T(8,128)(2,1)S(1)}, bf16[128,1024]{1,0:T(8,128)(2,1)}, u32[]{:S(2)}) copy-start(bf16[128,1024]{1,0:T(8,128)(2,1)} %param.9) | copy-start | bytes 786436
  23.6 416.9 %all-to-all-start = ((bf16[1024,32,128]{2,0,1:T(8,128)(2,1)}), bf16[1024,32,128]{2,0,1:T(8,128)(2,1)}, u32[]{:S(2)}, u32[]{:S(2)}) async-start(bf16[1024,32,128]{2,0,1:T(8,128)(2,1)} %copy.98), calls=%async_computation | async-start | bytes 16777216 | tf_op jit(solution)/shard_map/all_to_all | solution.py:13
  69.9 153.1 %all-gather.2.cloned.1.call-start = ((), (), s32[]{:S(2)}) async-start(), calls=%async_computation.2 | async-start | bytes 2162688 | tf_op jit(solution)/shard_map/all_gather | solution.py:22
Sparse Core Ops, SparseCore 0:
  72.8 150.1 all-gather.1
